TPU v7x, 512 devices: a whole 4x8x8 slice. The times are simulated.
512 devices in a mesh: gx: 8 (over y), gy: 64 (over x, z, core).
Axes of the slice: x: 4, y: 8, z: 8, core: 2. Of those that a mesh axis runs over, the one named last changes fastest.
Arguments:
- basis_mats: float32 [12, 275, 275], replicated, may hold values from -8 to 8.5, as said below
- coeffs: float32 [8192, 12], P(('gx', 'gy')), may hold values from 0.5 to 2
- element_loads: float32 [8192, 275], P(('gx', 'gy')), may hold values from -18 to 18
- elem_faces: int32 [8192, 6], P(('gx', 'gy')), may hold values from 0 to 71, as said below
- orient_codes: int32 [8192, 6], P(('gx', 'gy')), may hold values from 0 to 7
- shared_owned: int32 [512, 2, 4], P(('gx', 'gy')), may hold values from 0 to 63, as said below
- shared_remote: int32 [512, 2, 4], P(('gx', 'gy')), may hold values from 0 to 7, as said below
- lower_peers: int32 [512, 2], P(('gx', 'gy')), may hold values from 0 to 511, as said below
- upper_peers: int32 [512, 2], P(('gx', 'gy')), may hold values from 0 to 511, as said below
Outputs:
- trace: float32 [25, 32768], P(None, ('gx', 'gy'))
- residual: float32 [25, 32768], P(None, ('gx', 'gy'))
Inputs may be any that keep to these rules, and one draw needn't show every extreme that they name: `basis_mats`: each matrix is symmetric with every eigenvalue at least 0.5. `elem_faces`: an entry below 64 is a face slot that the element's device owns; an entry 64 + r is that device's remote slot r. Every owned slot of a device is named by one or two of its element faces, every remote slot by exactly one. `shared_owned`: row (d, i) lists 4 distinct owned slots of device d, in message order, that device lower_peers[d, i] uses; the two rows of a device are disjoint. `shared_remote`: row (d, i) lists remote slots of device d in message order: its k-th entry is the face that device upper_peers[d, i] lists k-th in its row i of shared_owned. The two rows of a device together hold each of its 8 remote slots once. upper_peers[lower_peers[d, i], i] = d for every device d and i; the two entries of a row differ. Peers are arbitrary device numbers. lower_peers[upper_peers[d, i], i] = d for every device d and i; the two entries of a row differ; each column is a permutation of the devices. Peers are arbitrary device numbers.
All inputs are finite; a program needn't handle non-finite values.
Results may differ from a plain program's by a relative error of at most 0.0003.
Values sent between devices are 32-bit elements; how exact they have to be, the bound alone decides.
No kernel may reach another device: no remote copies, remote signals or barrier semaphores. Data moves between devices by JAX's collectives and lax.ppermute only.
A program may use at most 128 MiB of HBM per device.

v0:
```python
import math
import jax
import jax.numpy as jnp
import numpy as np
from jax import lax
from jax.sharding import PartitionSpec as P

SIDE = 5
FACE_DOFS = 25
CELL_DOFS = 125
TRACE_DOFS = 150
ITERS = 4
FACE_DEV = 64
SHARED = 4
REMOTE = 8
full_precision = lax.Precision.HIGHEST


def orient_table():
    edge_nodes = SIDE
    codes_table = np.zeros((8, edge_nodes * edge_nodes), np.int32)
    for code_index in range(8):
        for first_axis in range(edge_nodes):
            for second_axis in range(edge_nodes):
                if code_index & 1:
                    first_new, second_new = (second_axis, first_axis)
                else:
                    first_new, second_new = (first_axis, second_axis)
                if code_index & 2:
                    first_new = edge_nodes - 1 - first_new
                if code_index & 4:
                    second_new = edge_nodes - 1 - second_new
                codes_table[code_index, first_axis * edge_nodes + second_axis] = (
                    first_new * edge_nodes + second_new
                )
    return codes_table


def permute_mats():
    codes_table = orient_table()
    matrices = np.zeros((8, FACE_DOFS, FACE_DOFS), np.float32)
    for code_index in range(8):
        for position in range(FACE_DOFS):
            matrices[code_index, position, codes_table[code_index, position]] = 1.0
    return matrices


def condense(coeffs, element_loads, basis_mats):
    element_mats = jnp.einsum("ek,kab->eab", coeffs, basis_mats, precision=full_precision)
    inner_block = element_mats[:, :CELL_DOFS, :CELL_DOFS]
    coupling = element_mats[:, :CELL_DOFS, CELL_DOFS:]
    outer_block = element_mats[:, CELL_DOFS:, CELL_DOFS:]
    factor = jnp.linalg.cholesky(inner_block)
    solved = jax.scipy.linalg.solve_triangular(factor, coupling, lower=True)
    source = jax.scipy.linalg.solve_triangular(
        factor, element_loads[:, :CELL_DOFS, None], lower=True
    )[:, :, 0]
    schur_part = outer_block - jnp.einsum("eib,eic->ebc", solved, solved, precision=full_precision)
    load_trace = element_loads[:, CELL_DOFS:] - jnp.einsum(
        "eib,ei->eb", solved, source, precision=full_precision
    )
    return (schur_part, load_trace)


def condense_blocks(coeffs, element_loads, basis_mats):
    elem_count = coeffs.shape[0]
    block_rows = math.gcd(elem_count, 16)
    grouped = (
        coeffs.reshape(-1, block_rows, coeffs.shape[1]),
        element_loads.reshape(-1, block_rows, element_loads.shape[1]),
    )
    schur_part, load_trace = lax.map(
        lambda pieces: condense(pieces[0], pieces[1], basis_mats), grouped
    )
    return (
        schur_part.reshape(elem_count, TRACE_DOFS, TRACE_DOFS),
        load_trace.reshape(elem_count, TRACE_DOFS),
    )


def pick_columns(fields, columns):
    picked = fields[:, :, columns]
    return jnp.moveaxis(picked, 2, 0).reshape(2, -1)


def place_rows(fields, columns, arrived):
    shaped = jnp.moveaxis(arrived.reshape(2, fields.shape[0], FACE_DOFS, SHARED), 0, 2)
    return fields.at[:, :, columns].add(shaped)


def owned_dot(first, second):
    return jnp.sum(first * second)


def on_device(
    basis_mats,
    coeffs,
    element_loads,
    elem_faces,
    orient_codes,
    shared_owned,
    shared_remote,
    lower_peers,
    upper_peers,
):
    elem_count = coeffs.shape[0]
    extent = FACE_DEV + REMOTE
    size_outer = lax.axis_size("gx")
    size_inner = lax.axis_size("gy")
    devices = size_outer * size_inner
    schur_blocks, load_trace = condense_blocks(coeffs, element_loads, basis_mats)
    choose = (orient_codes[:, :, None] == jnp.arange(8, dtype=jnp.int32)[None, None, :]).astype(
        jnp.float32
    )
    permute = jnp.einsum(
        "ejo,oqp->ejqp", choose, jnp.asarray(permute_mats()), precision=full_precision
    )
    incidence = (
        elem_faces.reshape(-1)[:, None] == jnp.arange(extent, dtype=jnp.int32)[None, :]
    ).astype(jnp.float32)
    owned_lists = shared_owned[0]
    remote_lists = FACE_DEV + shared_remote[0]
    lower_ids = lower_peers[0]
    upper_ids = upper_peers[0]

    def collect(element_values):
        shaped = element_values.reshape(elem_count, 6, FACE_DOFS)
        placed = jnp.einsum("ejqp,ejq->ejp", permute, shaped, precision=full_precision)
        return jnp.dot(
            placed.reshape(elem_count * 6, FACE_DOFS).T, incidence, precision=full_precision
        )

    fields = jnp.stack([collect(load_trace), collect(jnp.diagonal(schur_blocks, axis1=1, axis2=2))])

    def upward_bucket(partial_value):
        outgoing = pick_columns(partial_value, remote_lists)
        bucket = jnp.zeros((devices, outgoing.shape[1]), jnp.float32).at[upper_ids].set(outgoing)
        return bucket.reshape(size_outer, size_inner, -1)

    def upward_settle(partial_value, arrived):
        incoming = arrived.reshape(devices, -1)[lower_ids]
        return place_rows(partial_value[:, :, :FACE_DEV], owned_lists, incoming)

    def downward_bucket(values):
        outgoing = pick_columns(values[None], owned_lists)
        bucket = jnp.zeros((devices, outgoing.shape[1]), jnp.float32).at[lower_ids].set(outgoing)
        return bucket.reshape(size_outer, size_inner, -1)

    arrived = lax.all_to_all(
        lax.all_to_all(upward_bucket(fields), "gx", split_axis=0, concat_axis=0, tiled=True),
        "gy",
        split_axis=1,
        concat_axis=1,
        tiled=True,
    )
    settled = upward_settle(fields, arrived)
    rhs_faces = settled[0]
    diag_faces = settled[1]

    def rz_total(residual, precond):
        return lax.psum(owned_dot(residual, precond), ("gx", "gy"))

    trace = jnp.zeros_like(rhs_faces)
    residual = rhs_faces
    precond = residual / diag_faces
    direction = precond
    rz_now = rz_total(residual, precond)
    for iteration in range(ITERS):
        fetched = lax.all_to_all(
            lax.all_to_all(
                downward_bucket(direction), "gx", split_axis=0, concat_axis=0, tiled=True
            ),
            "gy",
            split_axis=1,
            concat_axis=1,
            tiled=True,
        )
        downward_incoming = fetched.reshape(devices, -1)[upper_ids]
        remote = place_rows(
            jnp.zeros((1, FACE_DOFS, REMOTE), jnp.float32), shared_remote[0], downward_incoming
        )
        gathered = jnp.dot(
            incidence, jnp.concatenate([direction, remote[0]], axis=1).T, precision=full_precision
        ).reshape(elem_count, 6, FACE_DOFS)
        operate_partial_value = collect(
            jnp.einsum(
                "ekl,el->ek",
                schur_blocks,
                jnp.einsum("ejqp,ejp->ejq", permute, gathered, precision=full_precision).reshape(
                    elem_count, TRACE_DOFS
                ),
                precision=full_precision,
            )
        )[None]
        returned = lax.all_to_all(
            lax.all_to_all(
                upward_bucket(operate_partial_value), "gx", split_axis=0, concat_axis=0, tiled=True
            ),
            "gy",
            split_axis=1,
            concat_axis=1,
            tiled=True,
        )
        mapped = upward_settle(operate_partial_value, returned)[0]
        step_size = rz_now / lax.psum(owned_dot(direction, mapped), ("gx", "gy"))
        trace = trace + step_size * direction
        residual = residual - step_size * mapped
        if iteration + 1 < ITERS:
            precond = residual / diag_faces
            rz_next = rz_total(residual, precond)
            direction = precond + rz_next / rz_now * direction
            rz_now = rz_next
    return (trace, residual)


def solution(mesh):
    placed = (
        P(),
        P(("gx", "gy"), None),
        P(("gx", "gy"), None),
        P(("gx", "gy"), None),
        P(("gx", "gy"), None),
        P(("gx", "gy"), None, None),
        P(("gx", "gy"), None, None),
        P(("gx", "gy"), None),
        P(("gx", "gy"), None),
    )
    return jax.shard_map(
        on_device,
        mesh=mesh,
        in_specs=placed,
        out_specs=(P(None, ("gx", "gy")), P(None, ("gx", "gy"))),
        check_vma=False,
    )
```

profile of v0, /device:TPU:1, one launch (start us, length us, event | category | flops | bytes accessed | tf_op | source)
XLA Modules:
  0.0 1485.4 jit_solution(4220468989809825634)
XLA Ops:
  1.3 9.7 fusion
  11.2 2.7 copy-done.2
  13.9 1.9 triangular_solve.47
  16.7 183.1 %custom-call.13 = f32[16,125,125]{2,1,0:T(8,128)S(1)} custom-call(f32[16,125,125]{2,1,0:T(8,128)S(1)} %fusion.20), custom_call_target="Cholesky" | custom-call | tf_op jit(solution)/shard_map/while/body/eval_jaxpr/jit(cholesky)/cholesky | solution.py:53
  200.3 153.7 %custom-call.14 = f32[16,1,125,125]{2,3,1,0:T(8,128)S(1)} custom-call(f32[16,1,125,125]{3,2,1,0:T(8,128)S(1)} %select_bitcast_fusion), custom_call_target="InvertDiagBlocksLowerTriangular" | custom-call | tf_op jit(solution)/shard_map/while/body/eval_jaxpr/jit(_solve_triangular)/vmap()/triangular_solve | solution.py:54
  354.0 5.9 fusion.10
  360.9 3.6 fusion.94
  364.5 2.0 fusion.92
  366.8 1.7 fusion.61
  368.5 2.1 copy.342
  370.6 2.5 fusion.93
  373.3 3.9 slice_subtract_fusion
  377.3 6.7 copy.270
  384.0 6.0 gather_fusion
  390.1 4.0 fusion.95
  396.4 22.3 %all_to_all.90 = f32[8,64,200]{2,1,0:T(8,128)S(1)} all-to-all(f32[8,64,200]{2,1,0:T(8,128)S(1)} %bitcast.301), channel_id=1, replica_groups=mesh['gx'=8,'gy'=64] {'gx'}, dimensions={0} | all-to-all | bytes 819200 | tf_op jit(solution)/shard_map/all_to_all | solution.py:150
  418.7 1.1 copy.275
  419.8 16.9 %all-to-all-start.1 = ((f32[8,64,200]{2,0,1:T(8,128)}), f32[8,64,200]{2,0,1:T(8,128)S(1)}, u32[]{:S(2)}, u32[]{:S(2)}) async-start(f32[8,64,200]{2,0,1:T(8,128)} %copy.275), calls=%async_computation.1 | async-start | bytes 1048576 | tf_op jit(solution)/shard_map/all_to_all | solution.py:149
  437.0 17.0 %all-to-all-done.1 = f32[8,64,200]{2,0,1:T(8,128)S(1)} async-done(((f32[8,64,200]{2,0,1:T(8,128)}), f32[8,64,200]{2,0,1:T(8,128)S(1)}, u32[]{:S(2)}, u32[]{:S(2)}) %all-to-all-start.1) | async-done | bytes 409632 | tf_op jit(solution)/shard_map/all_to_all | solution.py:149
  455.0 1.6 gather_fusion.2
  459.1 14.8 all_to_all.91
  474.8 6.1 all-to-all-start.3
  481.1 11.8 all-to-all-done.3
  493.7 1.0 scatter_custom_fusion.3
  495.0 4.1 fusion.16
  499.2 3.6 fusion.8
  502.9 4.0 fusion.96
  508.7 14.6 all_to_all.92
  524.2 6.1 all-to-all-start.5
  530.4 11.9 all-to-all-done.5
  544.3 95.6 %all-reduce = (f32[]{:T(128)}, f32[]{:T(128)}) all-reduce(f32[]{:T(128)} %get-tuple-element.33, f32[]{:T(128)} %get-tuple-element.32), channel_id=1, replica_groups=mesh['gx'=8,'gy'=64] {'gx','gy'}, use_global_device_ids=true, to_apply=%region_5.6 | all-reduce | flops 2 | bytes 16 | tf_op jit(solution)/shard_map/psum | solution.py:161
  641.8 93.4 %psum.58 = f32[]{:T(128)} all-reduce(f32[]{:T(128)} %get-tuple-element.44), channel_id=1, replica_groups=mesh['gx'=8,'gy'=64] {'gx','gy'}, use_global_device_ids=true, to_apply=%region_13.14 | all-reduce | flops 1 | bytes 8 | tf_op jit(solution)/shard_map/psum | solution.py:161
  738.1 15.0 %all_to_all.93 = f32[8,64,100]{2,1,0:T(8,128)S(1)} all-to-all(f32[8,64,100]{2,1,0:T(8,128)S(1)} %bitcast.307), channel_id=1, replica_groups=mesh['gx'=8,'gy'=64] {'gx'}, dimensions={0} | all-to-all | bytes 409600 | tf_op jit(solution)/shard_map/all_to_all | solution.py:170
  753.9 8.2 all-to-all-start.7
  762.2 11.9 all-to-all-done.7
  775.8 4.1 fusion.14
  780.0 3.6 fusion.6
  783.7 4.0 fusion.97
  789.5 14.6 all_to_all.94
  805.0 6.1 all-to-all-start.9
  811.2 11.9 all-to-all-done.9
  825.1 95.5 %psum.59 = f32[]{:T(128)} all-reduce(f32[]{:T(128)} %multiply_reduce_fusion.4), channel_id=1, replica_groups=mesh['gx'=8,'gy'=64] {'gx','gy'}, use_global_device_ids=true, to_apply=%region_19.20 | all-reduce | flops 1 | bytes 8 | tf_op jit(solution)/shard_map/psum | solution.py:205
  922.6 93.9 %psum.60 = f32[]{:T(128)} all-reduce(f32[]{:T(128)} %get-tuple-element.40), channel_id=1, replica_groups=mesh['gx'=8,'gy'=64] {'gx','gy'}, use_global_device_ids=true, to_apply=%region_21.22 | all-reduce | flops 1 | bytes 8 | tf_op jit(solution)/shard_map/psum | solution.py:161
  1019.3 14.9 %all_to_all.95 = f32[8,64,100]{2,1,0:T(8,128)S(1)} all-to-all(f32[8,64,100]{2,1,0:T(8,128)S(1)} %bitcast.309), channel_id=1, replica_groups=mesh['gx'=8,'gy'=64] {'gx'}, dimensions={0} | all-to-all | bytes 409600 | tf_op jit(solution)/shard_map/all_to_all | solution.py:170
  1035.1 8.0 all-to-all-start.11
  1043.2 11.9 all-to-all-done.11
  1056.8 4.1 fusion.12
  1061.1 3.6 fusion.4
  1064.8 4.0 fusion.98
  1070.5 14.6 all_to_all.96
  1086.0 6.1 all-to-all-start.13
  1092.2 11.9 all-to-all-done.13
  1106.3 95.5 %psum.61 = f32[]{:T(128)} all-reduce(f32[]{:T(128)} %multiply_reduce_fusion.2), channel_id=1, replica_groups=mesh['gx'=8,'gy'=64] {'gx','gy'}, use_global_device_ids=true, to_apply=%region_27.28 | all-reduce | flops 1 | bytes 8 | tf_op jit(solution)/shard_map/psum | solution.py:205
  1203.8 93.5 %psum.62 = f32[]{:T(128)} all-reduce(f32[]{:T(128)} %get-tuple-element.36), channel_id=1, replica_groups=mesh['gx'=8,'gy'=64] {'gx','gy'}, use_global_device_ids=true, to_apply=%region_29.30 | all-reduce | flops 1 | bytes 8 | tf_op jit(solution)/shard_map/psum | solution.py:161
  1300.2 14.9 %all_to_all.97 = f32[8,64,100]{2,1,0:T(8,128)S(1)} all-to-all(f32[8,64,100]{2,1,0:T(8,128)S(1)} %bitcast.304), channel_id=1, replica_groups=mesh['gx'=8,'gy'=64] {'gx'}, dimensions={0} | all-to-all | bytes 409600 | tf_op jit(solution)/shard_map/all_to_all | solution.py:170
  1316.0 8.0 all-to-all-start.15
  1324.0 11.9 all-to-all-done.15
  1337.6 4.1 fusion.18
  1341.9 3.6 fusion.2
  1345.6 4.0 fusion.99
  1351.4 14.6 all_to_all.98
  1366.8 6.1 all-to-all-start.17
  1373.0 11.9 all-to-all-done.17
  1387.0 95.5 %psum.63 = f32[]{:T(128)} all-reduce(f32[]{:T(128)} %multiply_reduce_fusion), channel_id=1, replica_groups=mesh['gx'=8,'gy'=64] {'gx','gy'}, use_global_device_ids=true, to_apply=%region_35.36 | all-reduce | flops 1 | bytes 8 | tf_op jit(solution)/shard_map/psum | solution.py:205
  (219 shorter events, 47.8 us)
Async XLA Ops:
  0.6 0.7 copy-start
  11.1 2.8 copy-start.2
  354.0 5.9 slice-start
  360.9 5.6 copy-start.4
  360.9 5.9 copy-start.3
  360.9 5.9 copy-start.5
  370.6 2.7 copy-start.1
  370.6 2.6 copy-start.6
  384.0 10.7 copy-start.7
  384.0 11.7 copy-start.9
  396.4 40.5 %copy-start.8 = (s32[1,2,4]{2,1,0:T(2,128)S(1)}, s32[1,2,4]{2,1,0:T(2,128)}, u32[]{:S(2)}) copy-start(s32[1,2,4]{2,1,0:T(2,128)} %param.15) | copy-start | bytes 100
  396.4 40.6 %copy-start.10 = (s32[1,2]{1,0:T(1,128)S(1)}, s32[1,2]{1,0:T(1,128)}, u32[]{:S(2)}) copy-start(s32[1,2]{1,0:T(1,128)} %param.17) | copy-start | bytes 28
  419.8 34.2 %all-to-all-start.1 = ((f32[8,64,200]{2,0,1:T(8,128)}), f32[8,64,200]{2,0,1:T(8,128)S(1)}, u32[]{:S(2)}, u32[]{:S(2)}) async-start(f32[8,64,200]{2,0,1:T(8,128)} %copy.275), calls=%async_computation.1 | async-start | bytes 1048576 | tf_op jit(solution)/shard_map/all_to_all | solution.py:149
  474.8 18.1 %all-to-all-start.3 = ((f32[8,64,100]{2,0,1:T(8,128)}), f32[8,64,100]{2,0,1:T(8,128)S(1)}, u32[]{:S(2)}, u32[]{:S(2)}) async-start(f32[8,64,100]{2,0,1:T(8,128)} %copy.281), calls=%async_computation.3 | async-start | bytes 524288 | tf_op jit(solution)/shard_map/all_to_all | solution.py:169
  524.2 18.1 %all-to-all-start.5 = ((f32[8,64,100]{2,0,1:T(8,128)}), f32[8,64,100]{2,0,1:T(8,128)S(1)}, u32[]{:S(2)}, u32[]{:S(2)}) async-start(f32[8,64,100]{2,0,1:T(8,128)} %copy.289), calls=%async_computation.5 | async-start | bytes 524288 | tf_op jit(solution)/shard_map/all_to_all | solution.py:195
  753.9 20.1 %all-to-all-start.7 = ((f32[8,64,100]{2,0,1:T(8,128)}), f32[8,64,100]{2,0,1:T(8,128)S(1)}, u32[]{:S(2)}, u32[]{:S(2)}) async-start(f32[8,64,100]{2,0,1:T(8,128)} %copy.295), calls=%async_computation.7 | async-start | bytes 524288 | tf_op jit(solution)/shard_map/all_to_all | solution.py:169
  805.0 18.1 %all-to-all-start.9 = ((f32[8,64,100]{2,0,1:T(8,128)}), f32[8,64,100]{2,0,1:T(8,128)S(1)}, u32[]{:S(2)}, u32[]{:S(2)}) async-start(f32[8,64,100]{2,0,1:T(8,128)} %copy.303), calls=%async_computation.9 | async-start | bytes 524288 | tf_op jit(solution)/shard_map/all_to_all | solution.py:195
  1035.1 19.9 %all-to-all-start.11 = ((f32[8,64,100]{2,0,1:T(8,128)}), f32[8,64,100]{2,0,1:T(8,128)S(1)}, u32[]{:S(2)}, u32[]{:S(2)}) async-start(f32[8,64,100]{2,0,1:T(8,128)} %copy.309), calls=%async_computation.11 | async-start | bytes 524288 | tf_op jit(solution)/shard_map/all_to_all | solution.py:169
  1086.0 18.1 %all-to-all-start.13 = ((f32[8,64,100]{2,0,1:T(8,128)}), f32[8,64,100]{2,0,1:T(8,128)S(1)}, u32[]{:S(2)}, u32[]{:S(2)}) async-start(f32[8,64,100]{2,0,1:T(8,128)} %copy.317), calls=%async_computation.13 | async-start | bytes 524288 | tf_op jit(solution)/shard_map/all_to_all | solution.py:195
  1316.0 19.9 %all-to-all-start.15 = ((f32[8,64,100]{2,0,1:T(8,128)}), f32[8,64,100]{2,0,1:T(8,128)S(1)}, u32[]{:S(2)}, u32[]{:S(2)}) async-start(f32[8,64,100]{2,0,1:T(8,128)} %copy.322), calls=%async_computation.15 | async-start | bytes 524288 | tf_op jit(solution)/shard_map/all_to_all | solution.py:169
  1366.8 18.1 %all-to-all-start.17 = ((f32[8,64,100]{2,0,1:T(8,128)}), f32[8,64,100]{2,0,1:T(8,128)S(1)}, u32[]{:S(2)}, u32[]{:S(2)}) async-start(f32[8,64,100]{2,0,1:T(8,128)} %copy.330), calls=%async_computation.17 | async-start | bytes 524288 | tf_op jit(solution)/shard_map/all_to_all | solution.py:195
where the time goes:
time: 1500 us; the launch traced here: 1490 us
  blocking collectives  803 us (54%)
  other arithmetic  353 us (24%)
  waiting for transfers between devices  112 us (7%)
  matrix products  79.3 us (5%)
  starting transfers between devices  71.4 us (5%)
  local copies, waits for them, and re-layouts  55.5 us (4%)
    psum x4, blocking collectives, rz_total(): return lax.psum(owned_dot(residual, precond), ('gx', 'gy'))  376 us
    psum x3, blocking collectives, on_device(): step_size = rz_now / lax.psum(owned_dot(direction, mapped), ('gx', 'gy'))  286 us
    another operation x4, other arithmetic, condense(): factor = jnp.linalg.cholesky(inner_block)  183 us
    another operation x3, other arithmetic, condense(): solved = jax.scipy.linalg.solve_triangular(factor, coupling, lower=True)  154 us
    all_to_all x4, blocking collectives, on_device(): lax.all_to_all(downward_bucket(direction), 'gx', split_axis=0, concat_axi...  59.6 us
    all_to_all x4, blocking collectives, on_device(): lax.all_to_all(upward_bucket(operate_partial_value), 'gx', split_axis=0,...  58.5 us
    all_to_all x4, waiting for transfers between devices, on_device(): lax.all_to_all(lax.all_to_all(upward_bucket(operate_partial_value), 'gx',...  47.5 us
    all_to_all x4, waiting for transfers between devices, on_device(): lax.all_to_all(lax.all_to_all(downward_bucket(direction), 'gx', split_axi...  47.4 us
  transfers between devices with their start and end apart: 9, of which 9 were waited for; matrix products, arithmetic and copies ran while one was open for 0% of the time, Pallas kernels for 0%

commit v1 on v0

--- a/solution.py
+++ b/solution.py
@@ -4,6 +4,7 @@
 import numpy as np
 from jax import lax
 from jax.sharding import PartitionSpec as P
+from jax.lax import psum
 
 SIDE = 5
 FACE_DOFS = 25
@@ -202,7 +203,7 @@
             tiled=True,
         )
         mapped = upward_settle(operate_partial_value, returned)[0]
-        step_size = rz_now / lax.psum(owned_dot(direction, mapped), ("gx", "gy"))
+        step_size = rz_now / psum(psum(owned_dot(direction, mapped), "gy"), "gx")
         trace = trace + step_size * direction
         residual = residual - step_size * mapped
         if iteration + 1 < ITERS:

time: 1500 us -> 1770 us (1.18)
  blocking collectives: 803 us -> 1070 us
    psum x3 -> x8, blocking collectives: 286 us -> 544 us  [on_device(): step_size = rz_now / psum(psum(owned_dot(direction, mapped), 'gy'), 'gx')]
where the time goes in v1:
time: 1770 us; the launch traced here: 1750 us
  blocking collectives  1070 us (60%)
  other arithmetic  353 us (20%)
  waiting for transfers between devices  112 us (6%)
  matrix products  79.3 us (4%)
  starting transfers between devices  69.4 us (4%)
  local copies, waits for them, and re-layouts  55.5 us (3%)
    psum x8, blocking collectives, on_device(): step_size = rz_now / psum(psum(owned_dot(direction, mapped), 'gy'), 'gx')  544 us
    psum x4, blocking collectives, rz_total(): return lax.psum(owned_dot(residual, precond), ('gx', 'gy'))  390 us
    another operation x4, other arithmetic, condense(): factor = jnp.linalg.cholesky(inner_block)  183 us
    another operation x3, other arithmetic, condense(): solved = jax.scipy.linalg.solve_triangular(factor, coupling, lower=True)  154 us
    all_to_all x4, blocking collectives, on_device(): lax.all_to_all(downward_bucket(direction), 'gx', split_axis=0, concat_axi...  59.5 us
    all_to_all x4, blocking collectives, on_device(): lax.all_to_all(upward_bucket(operate_partial_value), 'gx', split_axis=0,...  58.5 us
    all_to_all x4, waiting for transfers between devices, on_device(): lax.all_to_all(lax.all_to_all(upward_bucket(operate_partial_value), 'gx',...  47.5 us
    all_to_all x4, waiting for transfers between devices, on_device(): lax.all_to_all(lax.all_to_all(downward_bucket(direction), 'gx', split_axi...  47.4 us
  transfers between devices with their start and end apart: 9, of which 9 were waited for; matrix products, arithmetic and copies ran while one was open for 0% of the time, Pallas kernels for 0%

profile of v1, /device:TPU:1, one launch (start us, length us, event | category | flops | bytes accessed | tf_op | source)
XLA Modules:
  0.0 1754.9 jit_solution(12861167341302439988)
XLA Ops:
  1.3 9.7 fusion
  11.2 2.7 copy-done.2
  16.7 183.1 %custom-call.13 = f32[16,125,125]{2,1,0:T(8,128)S(1)} custom-call(f32[16,125,125]{2,1,0:T(8,128)S(1)} %fusion.20), custom_call_target="Cholesky" | custom-call | tf_op jit(solution)/shard_map/while/body/eval_jaxpr/jit(cholesky)/cholesky | solution.py:54
  200.3 153.7 %custom-call.14 = f32[16,1,125,125]{2,3,1,0:T(8,128)S(1)} custom-call(f32[16,1,125,125]{3,2,1,0:T(8,128)S(1)} %select_bitcast_fusion), custom_call_target="InvertDiagBlocksLowerTriangular" | custom-call | tf_op jit(solution)/shard_map/while/body/eval_jaxpr/jit(_solve_triangular)/vmap()/triangular_solve | solution.py:55
  354.0 5.9 fusion.10
  360.9 3.6 fusion.94
  364.5 2.0 fusion.92
  368.5 2.1 copy.342
  370.6 2.5 fusion.93
  373.3 3.9 slice_subtract_fusion
  377.3 6.7 copy.270
  384.0 6.0 gather_fusion
  390.1 4.0 fusion.95
  396.4 22.3 %all_to_all.90 = f32[8,64,200]{2,1,0:T(8,128)S(1)} all-to-all(f32[8,64,200]{2,1,0:T(8,128)S(1)} %bitcast.301), channel_id=1, replica_groups=mesh['gx'=8,'gy'=64] {'gx'}, dimensions={0} | all-to-all | bytes 819200 | tf_op jit(solution)/shard_map/all_to_all | solution.py:151
  419.8 16.9 all-to-all-start.1
  437.0 17.0 all-to-all-done.1
  459.1 14.8 all_to_all.91
  474.8 6.1 all-to-all-start.3
  481.1 11.8 all-to-all-done.3
  495.0 4.1 fusion.16
  499.2 3.6 fusion.8
  502.9 4.0 fusion.96
  508.7 14.6 all_to_all.92
  524.2 6.1 all-to-all-start.5
  530.4 11.9 all-to-all-done.5
  544.3 124.5 %psum.85 = f32[]{:T(128)} all-reduce(f32[]{:T(128)} %get-tuple-element.32), channel_id=1, replica_groups=mesh['gx'=8,'gy'=64] {'gy'}, use_global_device_ids=true, to_apply=%region_11.12 | all-reduce | flops 1 | bytes 8 | tf_op jit(solution)/shard_map/psum | solution.py:206
  668.8 11.6 psum.86
  680.4 98.5 %psum.84 = f32[]{:T(128)} all-reduce(f32[]{:T(128)} %get-tuple-element.33), channel_id=1, replica_groups=mesh['gx'=8,'gy'=64] {'gx','gy'}, use_global_device_ids=true, to_apply=%region_5.6 | all-reduce | flops 1 | bytes 8 | tf_op jit(solution)/shard_map/psum | solution.py:162
  780.9 94.3 %psum.87 = f32[]{:T(128)} all-reduce(f32[]{:T(128)} %get-tuple-element.42), channel_id=1, replica_groups=mesh['gx'=8,'gy'=64] {'gx','gy'}, use_global_device_ids=true, to_apply=%region_14.15 | all-reduce | flops 1 | bytes 8 | tf_op jit(solution)/shard_map/psum | solution.py:162
  878.1 15.9 all_to_all.93
  894.8 7.0 all-to-all-start.7
  901.9 11.9 all-to-all-done.7
  915.6 4.1 fusion.14
  919.8 3.6 fusion.6
  923.5 4.0 fusion.97
  929.3 14.6 all_to_all.94
  944.8 6.1 all-to-all-start.9
  950.9 11.9 all-to-all-done.9
  964.9 124.5 %psum.88 = f32[]{:T(128)} all-reduce(f32[]{:T(128)} %multiply_reduce_fusion.4), channel_id=1, replica_groups=mesh['gx'=8,'gy'=64] {'gy'}, use_global_device_ids=true, to_apply=%region_20.21 | all-reduce | flops 1 | bytes 8 | tf_op jit(solution)/shard_map/psum | solution.py:206
  1089.4 11.6 psum.89
  1102.9 98.5 %psum.90 = f32[]{:T(128)} all-reduce(f32[]{:T(128)} %get-tuple-element.38), channel_id=1, replica_groups=mesh['gx'=8,'gy'=64] {'gx','gy'}, use_global_device_ids=true, to_apply=%region_23.24 | all-reduce | flops 1 | bytes 8 | tf_op jit(solution)/shard_map/psum | solution.py:162
  1204.3 14.5 all_to_all.95
  1219.7 7.5 all-to-all-start.11
  1227.3 11.9 all-to-all-done.11
  1240.9 4.1 fusion.12
  1245.1 3.6 fusion.4
  1248.8 4.0 fusion.98
  1254.6 14.6 all_to_all.96
  1270.1 6.1 all-to-all-start.13
  1276.3 11.9 all-to-all-done.13
  1290.3 124.5 %psum.91 = f32[]{:T(128)} all-reduce(f32[]{:T(128)} %multiply_reduce_fusion.2), channel_id=1, replica_groups=mesh['gx'=8,'gy'=64] {'gy'}, use_global_device_ids=true, to_apply=%region_29.30 | all-reduce | flops 1 | bytes 8 | tf_op jit(solution)/shard_map/psum | solution.py:206
  1414.7 11.6 psum.92
  1428.3 98.8 %psum.93 = f32[]{:T(128)} all-reduce(f32[]{:T(128)} %get-tuple-element.34), channel_id=1, replica_groups=mesh['gx'=8,'gy'=64] {'gx','gy'}, use_global_device_ids=true, to_apply=%region_32.33 | all-reduce | flops 1 | bytes 8 | tf_op jit(solution)/shard_map/psum | solution.py:162
  1529.9 14.3 all_to_all.97
  1545.1 7.5 all-to-all-start.15
  1552.7 11.9 all-to-all-done.15
  1566.3 4.1 fusion.18
  1570.6 3.6 fusion.2
  1574.3 4.0 fusion.99
  1580.0 14.6 all_to_all.98
  1595.5 6.1 all-to-all-start.17
  1601.7 11.9 all-to-all-done.17
  1615.7 124.5 %psum.94 = f32[]{:T(128)} all-reduce(f32[]{:T(128)} %multiply_reduce_fusion), channel_id=1, replica_groups=mesh['gx'=8,'gy'=64] {'gy'}, use_global_device_ids=true, to_apply=%region_38.39 | all-reduce | flops 1 | bytes 8 | tf_op jit(solution)/shard_map/psum | solution.py:206
  1740.1 11.6 psum.95
  (224 shorter events, 55.0 us)
Async XLA Ops:
  0.6 0.7 copy-start
  11.1 2.8 copy-start.2
  354.0 5.9 slice-start
  360.9 5.6 copy-start.4
  360.9 5.9 copy-start.3
  360.9 5.9 copy-start.5
  370.6 2.7 copy-start.1
  370.6 2.6 copy-start.6
  384.0 10.7 copy-start.7
  384.0 11.7 copy-start.9
  396.4 40.5 %copy-start.8 = (s32[1,2,4]{2,1,0:T(2,128)S(1)}, s32[1,2,4]{2,1,0:T(2,128)}, u32[]{:S(2)}) copy-start(s32[1,2,4]{2,1,0:T(2,128)} %param.15) | copy-start | bytes 100
  396.4 40.6 %copy-start.10 = (s32[1,2]{1,0:T(1,128)S(1)}, s32[1,2]{1,0:T(1,128)}, u32[]{:S(2)}) copy-start(s32[1,2]{1,0:T(1,128)} %param.17) | copy-start | bytes 28
  419.8 34.2 %all-to-all-start.1 = ((f32[8,64,200]{2,0,1:T(8,128)}), f32[8,64,200]{2,0,1:T(8,128)S(1)}, u32[]{:S(2)}, u32[]{:S(2)}) async-start(f32[8,64,200]{2,0,1:T(8,128)} %copy.275), calls=%async_computation.1 | async-start | bytes 1048576 | tf_op jit(solution)/shard_map/all_to_all | solution.py:150
  474.8 18.1 %all-to-all-start.3 = ((f32[8,64,100]{2,0,1:T(8,128)}), f32[8,64,100]{2,0,1:T(8,128)S(1)}, u32[]{:S(2)}, u32[]{:S(2)}) async-start(f32[8,64,100]{2,0,1:T(8,128)} %copy.281), calls=%async_computation.3 | async-start | bytes 524288 | tf_op jit(solution)/shard_map/all_to_all | solution.py:170
  524.2 18.1 %all-to-all-start.5 = ((f32[8,64,100]{2,0,1:T(8,128)}), f32[8,64,100]{2,0,1:T(8,128)S(1)}, u32[]{:S(2)}, u32[]{:S(2)}) async-start(f32[8,64,100]{2,0,1:T(8,128)} %copy.289), calls=%async_computation.5 | async-start | bytes 524288 | tf_op jit(solution)/shard_map/all_to_all | solution.py:196
  894.8 19.0 %all-to-all-start.7 = ((f32[8,64,100]{2,0,1:T(8,128)}), f32[8,64,100]{2,0,1:T(8,128)S(1)}, u32[]{:S(2)}, u32[]{:S(2)}) async-start(f32[8,64,100]{2,0,1:T(8,128)} %copy.295), calls=%async_computation.7 | async-start | bytes 524288 | tf_op jit(solution)/shard_map/all_to_all | solution.py:170
  944.8 18.1 %all-to-all-start.9 = ((f32[8,64,100]{2,0,1:T(8,128)}), f32[8,64,100]{2,0,1:T(8,128)S(1)}, u32[]{:S(2)}, u32[]{:S(2)}) async-start(f32[8,64,100]{2,0,1:T(8,128)} %copy.303), calls=%async_computation.9 | async-start | bytes 524288 | tf_op jit(solution)/shard_map/all_to_all | solution.py:196
  1219.7 19.5 %all-to-all-start.11 = ((f32[8,64,100]{2,0,1:T(8,128)}), f32[8,64,100]{2,0,1:T(8,128)S(1)}, u32[]{:S(2)}, u32[]{:S(2)}) async-start(f32[8,64,100]{2,0,1:T(8,128)} %copy.309), calls=%async_computation.11 | async-start | bytes 524288 | tf_op jit(solution)/shard_map/all_to_all | solution.py:170
  1270.1 18.1 %all-to-all-start.13 = ((f32[8,64,100]{2,0,1:T(8,128)}), f32[8,64,100]{2,0,1:T(8,128)S(1)}, u32[]{:S(2)}, u32[]{:S(2)}) async-start(f32[8,64,100]{2,0,1:T(8,128)} %copy.317), calls=%async_computation.13 | async-start | bytes 524288 | tf_op jit(solution)/shard_map/all_to_all | solution.py:196
  1545.1 19.5 %all-to-all-start.15 = ((f32[8,64,100]{2,0,1:T(8,128)}), f32[8,64,100]{2,0,1:T(8,128)S(1)}, u32[]{:S(2)}, u32[]{:S(2)}) async-start(f32[8,64,100]{2,0,1:T(8,128)} %copy.322), calls=%async_computation.15 | async-start | bytes 524288 | tf_op jit(solution)/shard_map/all_to_all | solution.py:170
  1595.5 18.1 %all-to-all-start.17 = ((f32[8,64,100]{2,0,1:T(8,128)}), f32[8,64,100]{2,0,1:T(8,128)S(1)}, u32[]{:S(2)}, u32[]{:S(2)}) async-start(f32[8,64,100]{2,0,1:T(8,128)} %copy.330), calls=%async_computation.17 | async-start | bytes 524288 | tf_op jit(solution)/shard_map/all_to_all | solution.py:196
